TPU v7x, 32 devices: a whole 2x2x4 slice. The times are simulated.
32 devices in a mesh: dp: 32 (over z, y, x, core), mp: 1.
Axes of the slice: x: 2, y: 2, z: 4, core: 2. Of those that a mesh axis runs over, the one named last changes fastest.
Arguments:
- gradients: bfloat16 [32, 512, 6144], P('dp', None, 'mp'), may hold values from -48 to 48
- weights: bfloat16 [512, 6144], P(None, 'mp'), may hold values from -3 to 3
- master: float32 [512, 6144], P('dp', 'mp'), may hold values from -6 to 6
- moment_one: float32 [512, 6144], P('dp', 'mp'), may hold values from -6 to 6
- moment_two: float32 [512, 6144], P('dp', 'mp'), may hold values from 0.25 to 4
- group_ids: int32 [512], replicated, may hold values from 0 to 15, never falling along the last dimension, each value on 1 to 64 neighbouring positions
Outputs:
- new_weights: bfloat16 [512, 6144], P(None, 'mp')
- new_master: float32 [512, 6144], P('dp', 'mp')
- new_first: float32 [512, 6144], P('dp', 'mp')
- new_second: float32 [512, 6144], P('dp', 'mp')
Inputs may be any that keep to these rules, and one draw needn't show every extreme that they name: `group_ids`: group numbers never fall along the rows; each group has 1 to 64 rows and every group is present.
All inputs are finite; a program needn't handle non-finite values.
Results may differ from a plain program's by a relative error of at most 0.001.
The roundings to bfloat16 on the way count: a program that leaves them out, or rounds other values in their place, can miss the bound.
Values may be sent and summed in bfloat16 or wider, within the bound.
A program may use at most 64 MiB of HBM per device.

v0:
```python
import jax
import jax.numpy as jnp
from jax import lax
from jax.sharding import PartitionSpec as P

beta_one = 0.9
beta_two = 0.999
adam_eps = 1e-06
weight_decay = 0.01
learn_rate = 0.04
step_count = 100


def on_device(gradients, weights, master, moment_one, moment_two, group_ids):
    owned_rows = master.shape[0]
    rows_all = weights.shape[0]
    groups = rows_all // 32
    replicas = lax.axis_size("dp")
    my_index = lax.axis_index("dp")
    first_own = my_index * owned_rows
    my_groups = lax.dynamic_slice_in_dim(group_ids, first_own, owned_rows, 0)
    member = (my_groups[:, None] == jnp.arange(groups, dtype=jnp.int32)[None, :]).astype(
        jnp.float32
    )
    weight_rows = jnp.dot(jnp.sum(master * master, axis=1), member, precision=lax.Precision.HIGHEST)
    local_grad = gradients[0]
    summed = lax.psum_scatter(local_grad.astype(jnp.float32), "dp", scatter_dimension=0, tiled=True)
    grad_mean = summed / replicas
    new_first = beta_one * moment_one + (1.0 - beta_one) * grad_mean
    new_second = beta_two * moment_two + (1.0 - beta_two) * grad_mean * grad_mean
    correct_one = 1.0 - beta_one**step_count
    correct_two = 1.0 - beta_two**step_count
    update = (
        new_first / correct_one / (jnp.sqrt(new_second / correct_two) + adam_eps)
        + weight_decay * master
    )
    update_rows = jnp.dot(jnp.sum(update * update, axis=1), member, precision=lax.Precision.HIGHEST)
    weight_sq, update_sq = lax.psum((weight_rows, update_rows), ("dp", "mp"))
    trust_ratio = jnp.sqrt(weight_sq / (update_sq + 1e-06))
    row_ratio = jnp.dot(member, trust_ratio, precision=lax.Precision.HIGHEST)
    step_size = learn_rate * row_ratio[:, None] * update
    new_master = master - step_size
    delta_bf = (-step_size).astype(jnp.bfloat16)
    new_weights = (
        weights.astype(jnp.float32)
        + lax.all_gather(delta_bf, "dp", axis=0, tiled=True).astype(jnp.float32)
    ).astype(jnp.bfloat16)
    return (new_weights, new_master, new_first, new_second)


def solution(mesh):
    placed = (P("dp", None, "mp"), P(None, "mp"), P("dp", "mp"), P("dp", "mp"), P("dp", "mp"), P())
    return jax.shard_map(
        on_device,
        mesh=mesh,
        in_specs=placed,
        out_specs=(P(None, "mp"), P("dp", "mp"), P("dp", "mp"), P("dp", "mp")),
        check_vma=False,
    )
```

profile of v0, /device:TPU:0, one launch (start us, length us, event | category | flops | bytes accessed | tf_op | source)
XLA Modules:
  0.0 302.7 jit_solution(6108356624688245434)
XLA Ops:
  7.2 0.0 reduce-scatter.2.cloned.1.call-start
  7.2 9.0 %bitcast_convert_fusion = f32[512,6144]{1,0:T(8,128)} fusion(bf16[1,512,6144]{2,1,0:T(8,128)(2,1)} %param.6), kind=kLoop, calls=%fused_computation.1 | loop fusion | flops 3145728 | bytes 18874368 | tf_op jit(solution)/shard_map/convert_element_type | solution.py:27
  16.2 0.0 copy-start
  16.2 0.0 copy-start.1
  16.2 0.0 copy-start.2
  16.2 0.0 reduce-scatter.2.cloned.1.call-update
  16.2 0.0 all-gather.2.cloned.1.call-start
  16.3 0.8 dynamic_slice.3
  17.1 156.8 %reduce-scatter.2.cloned.1.call-done = f32[16,6144]{1,0:T(8,128)} async-done(((f32[512,6144]{1,0:T(8,128)}), f32[16,6144]{1,0:T(8,128)}) %reduce-scatter.2.cloned.1.call-update) | async-done | bytes 393232 | tf_op jit(solution)/shard_map/reduce_scatter | solution.py:27
  174.0 0.0 copy-done
  174.0 0.0 copy-done.1
  174.0 0.0 copy-done.2
  174.0 2.3 multiply_reduce_fusion
  176.3 0.2 convolution_bitcast_fusion.1
  176.5 0.2 convolution_bitcast_fusion.2
  176.7 39.4 %all-reduce = (f32[16]{0:T(128)S(1)}, f32[16]{0:T(128)S(1)}) all-reduce(f32[16]{0:T(128)S(1)} %convolution_bitcast_fusion.2, f32[16]{0:T(128)S(1)} %convolution_bitcast_fusion.1), channel_id=1, replica_groups=mesh['dp'=32,'mp'=1] {'dp','mp'}, use_global_device_ids=true, to_apply=%region_1.0 | all-reduce | flops 32 | bytes 256 | tf_op jit(solution)/shard_map/psum | solution.py:38
  216.0 0.2 fusion
  216.2 0.9 multiply_subtract_fusion
  217.2 0.0 all-gather.2.cloned.1.call-update
  217.2 68.7 %all-gather.2.cloned.1.call-done = bf16[512,6144]{1,0:T(8,128)(2,1)} async-done(((bf16[16,6144]{1,0:T(8,128)(2,1)}), bf16[512,6144]{1,0:T(8,128)(2,1)}) %all-gather.2.cloned.1.call-update) | async-done | bytes 6291472 | tf_op jit(solution)/shard_map/all_gather | solution.py:46
  285.9 10.0 %add_convert_fusion = bf16[512,6144]{1,0:T(8,128)(2,1)} fusion(bf16[512,6144]{1,0:T(8,128)(2,1)} %all-gather.2.cloned.1.call-done, bf16[512,6144]{1,0:T(8,128)(2,1)} %param.7), kind=kLoop, calls=%fused_computation | loop fusion | flops 12582912 | bytes 18874368 | tf_op jit(solution)/shard_map/convert_element_type | solution.py:47
Async XLA Ops:
  7.2 166.8 %reduce-scatter.2.cloned.1.call-start = ((), (), s32[]{:S(2)}) async-start(), calls=%async_computation.1 | async-start | bytes 12976128 | tf_op jit(solution)/shard_map/reduce_scatter | solution.py:27
  16.2 157.8 %copy-start = (f32[16,6144]{1,0:T(8,128)S(1)}, f32[16,6144]{1,0:T(8,128)}, u32[]{:S(2)}) copy-start(f32[16,6144]{1,0:T(8,128)} %param.8) | copy-start | bytes 1179652
  16.2 157.8 %copy-start.1 = (f32[16,6144]{1,0:T(8,128)S(1)}, f32[16,6144]{1,0:T(8,128)}, u32[]{:S(2)}) copy-start(f32[16,6144]{1,0:T(8,128)} %param.9) | copy-start | bytes 1179652
  16.2 157.8 %copy-start.2 = (f32[16,6144]{1,0:T(8,128)S(1)}, f32[16,6144]{1,0:T(8,128)}, u32[]{:S(2)}) copy-start(f32[16,6144]{1,0:T(8,128)} %param.10) | copy-start | bytes 1179652
  16.2 269.7 %all-gather.2.cloned.1.call-start = ((), (), s32[]{:S(2)}) async-start(), calls=%async_computation.2 | async-start | bytes 6488064 | tf_op jit(solution)/shard_map/all_gather | solution.py:46
Sparse Core Ops, SparseCore 0:
  16.4 157.5 reduce-scatter.1
  217.3 68.5 all-gather.1
where the time goes:
time: 303 us
  waiting for transfers between devices  226 us (75%)
  blocking collectives  39.4 us (13%)
  other arithmetic  22.2 us (7%)
  between operations  14 us (5%)
    reduce_scatter x1, waiting for transfers between devices, on_device(): lax.psum_scatter(local_grad.astype(jnp.float32), 'dp', scatter_dimension=...  157 us
    all_gather x1, waiting for transfers between devices, on_device(): lax.all_gather(delta_bf, 'dp', axis=0, tiled=True).astype(jnp.float32)  68.7 us
    psum x1, blocking collectives, on_device(): weight_sq, update_sq = lax.psum((weight_rows, update_rows), ('dp', 'mp'))  39.4 us
    convert_element_type x1, other arithmetic, on_device(): new_weights = (weights.astype(jnp.float32) + lax.all_gather(delta_bf, 'dp...  9.96 us
    convert_element_type x1, other arithmetic, on_device(): local_grad.astype(jnp.float32)  8.99 us
  transfers between devices with their start and end apart: 2, of which 2 were waited for; matrix products, arithmetic and copies ran while one was open for 0% of the time, Pallas kernels for 0%

commit v1 on v0

v1 whole, which is shorter than its diff:
```python
import functools

import jax
import jax.numpy as jnp
from jax import lax
from jax.experimental import pallas as pl
from jax.experimental.pallas import tpu as pltpu
from jax.sharding import PartitionSpec as P

beta_one = 0.9
beta_two = 0.999
adam_eps = 1e-06
weight_decay = 0.01
learn_rate = 0.04
step_count = 100

MESH = pl.DeviceIdType.MESH
F32, BF16 = jnp.float32, jnp.bfloat16
WIDTH = 512


def flipped(bit, flag):
    return bit + flag - 2 * bit * flag


def kernel(
    n, mp, width, ids_ref, grad_ref, w_ref, master_ref, m1_ref, m2_ref,
    out_ref, new_master_ref, new_first_ref, new_second_ref,
    mine, raw, acc, recvs, weights, held, update, member, tiles,
    mine_sem, w_sem, out_sem, rs_send, rs_recv, ag_send, ag_recv, t_send, t_recv,
):
    me = lax.axis_index("dp")
    bits = [(me // 2**i) % 2 for i in range(n)]
    replicas = 2**n
    rows, cols = master_ref.shape
    chunks = cols // width
    units = [list(range(j, min(j + 2, chunks))) for j in range(0, chunks, 2)]
    orders = []
    for k in range(chunks):
        order = list(range(n))
        if k % 2 and n > 2:
            order[1], order[2] = order[2], order[1]
        orders.append(order)

    def span(k):
        return pl.ds(k * width, width)

    def partner(flips):
        return sum(2**i * (1 - bits[i] if flips >> i & 1 else bits[i]) for i in range(n))

    low = min(n, 3)
    levels = [[{"dp": partner(f)} for f in range(1, 2**low)]]
    if n > low:
        levels.append([{"dp": partner(f << low)} for f in range(1, 2 ** (n - low))])
    if mp > 1:
        mine_mp = lax.axis_index("mp")
        places = mp.bit_length() - 1
        mp_bits = [(mine_mp // 2**i) % 2 for i in range(places)]
        levels.append([
            {"mp": sum(2**i * (1 - mp_bits[i] if f >> i & 1 else mp_bits[i]) for i in range(places))}
            for f in range(1, mp)
        ])

    w_copy = pltpu.make_async_copy(w_ref, weights, w_sem)
    mine_copies = [
        pltpu.make_async_copy(grad_ref.at[:, bits[0], :, span(k)], mine.at[k], mine_sem.at[k])
        for k in range(chunks)
    ]
    for copy in mine_copies:
        copy.start()

    barrier = pltpu.get_barrier_semaphore()
    greeted = [target for level in levels for target in level]
    for target in greeted:
        pl.semaphore_signal(barrier, inc=1, device_id=target, device_id_type=MESH)
    pl.semaphore_wait(barrier, len(greeted))

    started = []

    def send(src, dst, send_sem, recv_sem, target):
        copy = pltpu.make_async_remote_copy(
            src_ref=src, dst_ref=dst, send_sem=send_sem, recv_sem=recv_sem,
            device_id=target, device_id_type=MESH,
        )
        copy.start()
        started.append(copy)
        return copy

    rs = {}
    for k in range(chunks):
        rs[k, 0] = send(
            grad_ref.at[:, 1 - bits[0], :, span(k)], raw.at[k],
            rs_send.at[k, 0], rs_recv.at[k, 0], {"dp": partner(1)},
        )
    w_copy.start()

    lanes = member.shape[1]
    lane = lax.broadcasted_iota(jnp.int32, (rows, lanes), 1)
    row = lax.broadcasted_iota(jnp.int32, (rows, lanes), 0)
    own_ids = jnp.zeros((rows, lanes), jnp.int32)
    for r in range(rows):
        own_ids = jnp.where(row == r, ids_ref[me * rows + r], own_ids)
    member[...] = jnp.where(lane == own_ids, 1.0, 0.0).astype(F32)

    row_sums = {"w": jnp.zeros((rows, 1), F32), "u": jnp.zeros((rows, 1), F32)}
    correct_one = 1.0 - beta_one**step_count
    correct_two = 1.0 - beta_two**step_count

    def advance(k, s):
        order = orders[k]
        rs[k, s].wait_recv()
        if s == 0:
            mine_copies[k].wait()

            @pl.loop(0, 2 ** (n - 1))
            def _(d):
                rest = 0
                for i in range(n - 1):
                    b = order[n - 1 - i]
                    rest = rest + 2 ** (b - 1) * flipped(bits[b], (d // 2**i) % 2)
                acc[k, d] = mine[k, rest].astype(F32) + raw[k, rest].astype(F32)
            total = acc
        else:
            before = acc if s == 1 else recvs[s - 2]
            total = recvs[s - 1]

            @pl.loop(0, 2 ** (n - 1 - s))
            def _(d):
                total[k, d] = total[k, d] + before[k, d]
        if s < n - 1:
            half = 2 ** (n - 2 - s)
            rs[k, s + 1] = send(
                total.at[k, pl.ds(half, half)], recvs[s].at[k],
                rs_send.at[k, s + 1], rs_recv.at[k, s + 1],
                {"dp": partner(1 << order[s + 1])},
            )
            return
        grad_mean = total[k, 0] / replicas
        master = master_ref[:, span(k)]
        new_first = beta_one * m1_ref[:, span(k)] + (1.0 - beta_one) * grad_mean
        new_second = beta_two * m2_ref[:, span(k)] + (1.0 - beta_two) * grad_mean * grad_mean
        new_first_ref[:, span(k)] = new_first
        new_second_ref[:, span(k)] = new_second
        change = (
            new_first / correct_one / (jnp.sqrt(new_second / correct_two) + adam_eps)
            + weight_decay * master
        )
        update[:, span(k)] = change
        row_sums["w"] += jnp.sum(master * master, axis=1, keepdims=True)
        row_sums["u"] += jnp.sum(change * change, axis=1, keepdims=True)

    for t in range(len(units) + n - 1):
        for s in range(n):
            if 0 <= t - s < len(units):
                for k in units[t - s]:
                    advance(k, s)

    w_part = jnp.sum(member[...] * row_sums["w"], axis=0, keepdims=True)
    u_part = jnp.sum(member[...] * row_sums["u"], axis=0, keepdims=True)
    sub = lax.broadcasted_iota(jnp.int32, (8, lanes), 0)
    sums = jnp.where(sub == 0, w_part, u_part)
    at = 0
    for level, slots in zip(levels, tiles):
        slots[0] = sums
        copies = []
        for f, target in enumerate(level, 1):
            copies.append(send(slots.at[0], slots.at[f], t_send.at[at], t_recv.at[at], target))
            at += 1
        for f, copy in enumerate(copies, 1):
            copy.wait_recv()
            sums = sums + slots[f]
    trust = jnp.sqrt(sums[0:1] / (sums[1:2] + 1e-06))
    row_ratio = jnp.sum(member[...] * trust, axis=1, keepdims=True)
    scale = learn_rate * row_ratio

    ag = {}

    def gather(k, s):
        ag[k, s] = send(
            held.at[k, pl.ds(0, 2**s)], held.at[k, pl.ds(2**s, 2**s)],
            ag_send.at[k, s], ag_recv.at[k, s], {"dp": partner(1 << orders[k][n - 1 - s])},
        )

    for k in range(chunks):
        step = scale * update[:, span(k)]
        held[k, 0] = (-step).astype(BF16)
        gather(k, 0)
        new_master_ref[:, span(k)] = master_ref[:, span(k)] - step
    w_copy.wait()

    def apply(k, first, count):
        @pl.loop(first, first + count)
        def _(d):
            owner = 0
            for i in range(n):
                b = orders[k][n - 1 - i]
                owner = owner + 2**b * flipped(bits[b], (d // 2**i) % 2)
            weights[owner, :, span(k)] = (
                weights[owner, :, span(k)].astype(F32) + held[k, d].astype(F32)
            ).astype(BF16)

    outs = []
    for t in range(len(units) + n - 1):
        for s in range(n):
            if 0 <= t - s < len(units):
                for k in units[t - s]:
                    ag[k, s].wait_recv()
                    if s < n - 1:
                        gather(k, s + 1)
                    if s == n - 2:
                        apply(k, 0, 2 ** (n - 1))
                    elif s == n - 1:
                        apply(k, 2 ** (n - 1), 2 ** (n - 1))
                        copy = pltpu.make_async_copy(
                            weights.at[:, :, span(k)], out_ref.at[:, :, span(k)], out_sem.at[k]
                        )
                        copy.start()
                        outs.append(copy)
    for copy in started:
        copy.wait_send()
    for copy in outs:
        copy.wait()


def solution(mesh):
    replicas, mp = mesh.shape["dp"], mesh.shape["mp"]
    n = replicas.bit_length() - 1

    def on_device(gradients, weights, master, moment_one, moment_two, group_ids):
        rows_all, cols = weights.shape
        rows = master.shape[0]
        width = WIDTH if cols % WIDTH == 0 else 128
        chunks = cols // width
        groups = rows_all // 32
        lanes = -(-groups // 128) * 128
        low = min(n, 3)
        counts = [2**low] + ([2 ** (n - low)] if n > low else []) + ([mp] if mp > 1 else [])
        anywhere = pl.BlockSpec(memory_space=pl.ANY)
        vmem = pl.BlockSpec(memory_space=pltpu.VMEM)
        own = jax.ShapeDtypeStruct((rows, cols), F32)
        dma = pltpu.SemaphoreType.DMA
        tiles_n = sum(c - 1 for c in counts)
        new_weights, new_master, new_first, new_second = pl.pallas_call(
            functools.partial(kernel, n, mp, width),
            out_shape=(jax.ShapeDtypeStruct((replicas, rows, cols), BF16), own, own, own),
            in_specs=[pl.BlockSpec(memory_space=pltpu.SMEM), anywhere, anywhere, vmem, vmem, vmem],
            out_specs=(anywhere, vmem, vmem, vmem),
            scratch_shapes=[
                pltpu.VMEM((chunks, replicas // 2, rows, width), BF16),
                pltpu.VMEM((chunks, replicas // 2, rows, width), BF16),
                pltpu.VMEM((chunks, replicas // 2, rows, width), F32),
                [pltpu.VMEM((chunks, 2 ** (n - 1 - s), rows, width), F32) for s in range(1, n)],
                pltpu.VMEM((replicas, rows, cols), BF16),
                pltpu.VMEM((chunks, replicas, rows, width), BF16),
                pltpu.VMEM((rows, cols), F32),
                pltpu.VMEM((rows, lanes), F32),
                [pltpu.VMEM((c, 8, lanes), F32) for c in counts],
                dma((chunks,)),
                dma,
                dma((chunks,)),
                dma((chunks, n)),
                dma((chunks, n)),
                dma((chunks, n)),
                dma((chunks, n)),
                dma((tiles_n,)),
                dma((tiles_n,)),
            ],
            compiler_params=pltpu.CompilerParams(
                collective_id=0, has_side_effects=True, vmem_limit_bytes=56 * 2**20
            ),
        )(
            group_ids,
            gradients.reshape(replicas // 2, 2, rows, cols),
            weights.reshape(replicas, rows, cols),
            master, moment_one, moment_two,
        )
        return new_weights.reshape(rows_all, cols), new_master, new_first, new_second

    return jax.shard_map(
        on_device,
        mesh=mesh,
        in_specs=(P("dp", None, "mp"), P(None, "mp"), P("dp", "mp"), P("dp", "mp"), P("dp", "mp"), P()),
        out_specs=(P(None, "mp"), P("dp", "mp"), P("dp", "mp"), P("dp", "mp")),
        check_vma=False,
    )
```

time: 303 us -> 134 us (0.44)
  waiting for transfers between devices: 226 us -> 0 us
  Pallas kernels: 0 us -> 125 us
  blocking collectives: 39.4 us -> 0 us
  other arithmetic: 22.2 us -> 0 us
  between operations: 14 us -> 0.67 us
  local copies, waits for them, and re-layouts: 0.85 us -> 8.58 us
    reduce_scatter x1 -> x0, waiting for transfers between devices: 157 us -> none  [on_device(): lax.psum_scatter(local_grad.astype(jnp.float32), 'dp', scatter_dimension=...]
    pallas_call x0 -> x1, Pallas kernels: none -> 125 us  [on_device(): pl.pallas_call(functools.partial(kernel, n, mp, width), out_shape=(jax.Sh...]
    all_gather x1 -> x0, waiting for transfers between devices: 68.7 us -> none  [on_device(): lax.all_gather(delta_bf, 'dp', axis=0, tiled=True).astype(jnp.float32)]
    psum x1 -> x0, blocking collectives: 39.4 us -> none  [on_device(): weight_sq, update_sq = lax.psum((weight_rows, update_rows), ('dp', 'mp'))]
    convert_element_type x2 -> x0, other arithmetic: 19 us -> none  [the longest x1 9.96 us: on_device(): new_weights = (weights.astype(jnp.float32) + lax.all_gather(delta_bf, 'dp...]
    unnamed x6 -> x10, local copies, waits for them, and re-layouts: 0.01 us -> 8.58 us
  transfers between devices with their start and end apart: 2 -> 0, of which waited for: 2 -> 0; matrix products, arithmetic and copies ran while one was open for 0% -> 0% of each run, Pallas kernels for 0% -> 0%
where the time goes in v1:
time: 134 us
  Pallas kernels  125 us (93%)
  local copies, waits for them, and re-layouts  8.58 us (6%)
    pallas_call x1, Pallas kernels, on_device(): pl.pallas_call(functools.partial(kernel, n, mp, width), out_shape=(jax.Sh...  125 us
    unnamed x10, local copies, waits for them, and re-layouts  8.58 us

profile of v1, /device:TPU:0, one launch (start us, length us, event | category | flops | bytes accessed | tf_op | source)
XLA Modules:
  0.0 133.9 jit_solution(5165534591686532313)
XLA Ops:
  0.6 124.7 %shard_map.93 = (bf16[32,16,6144]{2,1,0:T(8,128)(2,1)}, f32[16,6144]{1,0:T(8,128)}, f32[16,6144]{1,0:T(8,128)}, f32[16,6144]{1,0:T(8,128)}) custom-call(s32[512]{0:T(512)} %ids_ref.1, bf16[16,2,16,6144]{3,2,1,0:T(8,128)(2,1)} %bitcast.3, bf16[32,16,6144]{2,1,0:T(8,128)(2,1)} %bitcast.4, f32[16,6144]{1,0:T(8,128)} %master_ref.1, f32[16,6144]{1,0:T(8,128)} %m1_ref.1, ...), custom_call_target="tpu_custom_call" | custom-call | tf_op jit(solution)/shard_map/pallas_call | solution.py:243
  125.3 0.0 copy-start.2
  125.3 0.0 copy-start.1
  125.3 0.0 copy-start
  125.3 6.3 %copy.14 = bf16[512,6144]{1,0:T(8,128)(2,1)} copy(bf16[512,6144]{1,0:T(8,128)(2,1)} %bitcast.5) | data formatting | bytes 12582912
  131.7 0.0 copy-done.2
  131.7 0.7 copy.15
  132.4 0.0 copy-done.1
  132.4 0.7 copy.16
  133.2 0.0 copy-done
  133.2 0.7 copy.17
Async XLA Ops:
  125.3 6.4 %copy-start.2 = (f32[16,6144]{1,0:T(8,128)S(1)}, f32[16,6144]{1,0:T(8,128)}, u32[]{:S(2)}) copy-start(f32[16,6144]{1,0:T(8,128)} %get-tuple-element.17) | copy-start | bytes 1179652
  125.3 7.1 %copy-start.1 = (f32[16,6144]{1,0:T(8,128)S(1)}, f32[16,6144]{1,0:T(8,128)}, u32[]{:S(2)}) copy-start(f32[16,6144]{1,0:T(8,128)} %get-tuple-element.18) | copy-start | bytes 1179652
  125.3 7.8 %copy-start = (f32[16,6144]{1,0:T(8,128)S(1)}, f32[16,6144]{1,0:T(8,128)}, u32[]{:S(2)}) copy-start(f32[16,6144]{1,0:T(8,128)} %get-tuple-element.19) | copy-start | bytes 1179652

commit v2 on v1

--- a/solution.py
+++ b/solution.py
@@ -17,6 +17,9 @@
 MESH = pl.DeviceIdType.MESH
 F32, BF16 = jnp.float32, jnp.bfloat16
 WIDTH = 512
+SKEW = 2
+AG_SKEW = 2
+UNROLL = 4
 
 
 def flipped(bit, flag):
@@ -26,8 +29,8 @@
 def kernel(
     n, mp, width, ids_ref, grad_ref, w_ref, master_ref, m1_ref, m2_ref,
     out_ref, new_master_ref, new_first_ref, new_second_ref,
-    mine, raw, acc, recvs, weights, held, update, member, tiles,
-    mine_sem, w_sem, out_sem, rs_send, rs_recv, ag_send, ag_recv, t_send, t_recv,
+    mine, raw, acc, recvs, held, update, member, tiles,
+    mine_sem, w_sem, rs_send, rs_recv, ag_send, ag_recv, t_send, t_recv,
 ):
     me = lax.axis_index("dp")
     bits = [(me // 2**i) % 2 for i in range(n)]
@@ -38,8 +41,8 @@
     orders = []
     for k in range(chunks):
         order = list(range(n))
-        if k % 2 and n > 2:
-            order[1], order[2] = order[2], order[1]
+        if n > 3:
+            order[1:4] = [2, 3, 1] if k % 2 else [1, 3, 2]
         orders.append(order)
 
     def span(k):
@@ -61,7 +64,7 @@
             for f in range(1, mp)
         ])
 
-    w_copy = pltpu.make_async_copy(w_ref, weights, w_sem)
+    w_copy = pltpu.make_async_copy(w_ref, out_ref, w_sem)
     mine_copies = [
         pltpu.make_async_copy(grad_ref.at[:, bits[0], :, span(k)], mine.at[k], mine_sem.at[k])
         for k in range(chunks)
@@ -112,7 +115,7 @@
         if s == 0:
             mine_copies[k].wait()
 
-            @pl.loop(0, 2 ** (n - 1))
+            @pl.loop(0, 2 ** (n - 1), unroll=min(UNROLL, 2 ** (n - 1)))
             def _(d):
                 rest = 0
                 for i in range(n - 1):
@@ -124,7 +127,7 @@
             before = acc if s == 1 else recvs[s - 2]
             total = recvs[s - 1]
 
-            @pl.loop(0, 2 ** (n - 1 - s))
+            @pl.loop(0, 2 ** (n - 1 - s), unroll=min(UNROLL, 2 ** (n - 1 - s)))
             def _(d):
                 total[k, d] = total[k, d] + before[k, d]
         if s < n - 1:
@@ -149,10 +152,10 @@
         row_sums["w"] += jnp.sum(master * master, axis=1, keepdims=True)
         row_sums["u"] += jnp.sum(change * change, axis=1, keepdims=True)
 
-    for t in range(len(units) + n - 1):
+    for t in range(len(units) + SKEW * (n - 1)):
         for s in range(n):
-            if 0 <= t - s < len(units):
-                for k in units[t - s]:
+            if 0 <= t - SKEW * s < len(units):
+                for k in units[t - SKEW * s]:
                     advance(k, s)
 
     w_part = jnp.sum(member[...] * row_sums["w"], axis=0, keepdims=True)
@@ -189,21 +192,20 @@
     w_copy.wait()
 
     def apply(k, first, count):
-        @pl.loop(first, first + count)
+        @pl.loop(first, first + count, unroll=min(UNROLL, count))
         def _(d):
             owner = 0
             for i in range(n):
                 b = orders[k][n - 1 - i]
                 owner = owner + 2**b * flipped(bits[b], (d // 2**i) % 2)
-            weights[owner, :, span(k)] = (
-                weights[owner, :, span(k)].astype(F32) + held[k, d].astype(F32)
+            out_ref[owner, :, span(k)] = (
+                out_ref[owner, :, span(k)].astype(F32) + held[k, d].astype(F32)
             ).astype(BF16)
 
-    outs = []
-    for t in range(len(units) + n - 1):
+    for t in range(len(units) + AG_SKEW * (n - 1)):
         for s in range(n):
-            if 0 <= t - s < len(units):
-                for k in units[t - s]:
+            if 0 <= t - AG_SKEW * s < len(units):
+                for k in units[t - AG_SKEW * s]:
                     ag[k, s].wait_recv()
                     if s < n - 1:
                         gather(k, s + 1)
@@ -211,15 +213,8 @@
                         apply(k, 0, 2 ** (n - 1))
                     elif s == n - 1:
                         apply(k, 2 ** (n - 1), 2 ** (n - 1))
-                        copy = pltpu.make_async_copy(
-                            weights.at[:, :, span(k)], out_ref.at[:, :, span(k)], out_sem.at[k]
-                        )
-                        copy.start()
-                        outs.append(copy)
     for copy in started:
         copy.wait_send()
-    for copy in outs:
-        copy.wait()
 
 
 def solution(mesh):
@@ -237,27 +232,25 @@
         counts = [2**low] + ([2 ** (n - low)] if n > low else []) + ([mp] if mp > 1 else [])
         anywhere = pl.BlockSpec(memory_space=pl.ANY)
         vmem = pl.BlockSpec(memory_space=pltpu.VMEM)
-        own = jax.ShapeDtypeStruct((rows, cols), F32)
+        own = pltpu.VMEM((rows, cols), F32)
         dma = pltpu.SemaphoreType.DMA
         tiles_n = sum(c - 1 for c in counts)
         new_weights, new_master, new_first, new_second = pl.pallas_call(
             functools.partial(kernel, n, mp, width),
-            out_shape=(jax.ShapeDtypeStruct((replicas, rows, cols), BF16), own, own, own),
+            out_shape=(pltpu.VMEM((replicas, rows, cols), BF16), own, own, own),
             in_specs=[pl.BlockSpec(memory_space=pltpu.SMEM), anywhere, anywhere, vmem, vmem, vmem],
-            out_specs=(anywhere, vmem, vmem, vmem),
+            out_specs=(vmem, vmem, vmem, vmem),
             scratch_shapes=[
                 pltpu.VMEM((chunks, replicas // 2, rows, width), BF16),
                 pltpu.VMEM((chunks, replicas // 2, rows, width), BF16),
                 pltpu.VMEM((chunks, replicas // 2, rows, width), F32),
                 [pltpu.VMEM((chunks, 2 ** (n - 1 - s), rows, width), F32) for s in range(1, n)],
-                pltpu.VMEM((replicas, rows, cols), BF16),
                 pltpu.VMEM((chunks, replicas, rows, width), BF16),
                 pltpu.VMEM((rows, cols), F32),
                 pltpu.VMEM((rows, lanes), F32),
                 [pltpu.VMEM((c, 8, lanes), F32) for c in counts],
                 dma((chunks,)),
                 dma,
-                dma((chunks,)),
                 dma((chunks, n)),
                 dma((chunks, n)),
                 dma((chunks, n)),
@@ -266,7 +259,7 @@
                 dma((tiles_n,)),
             ],
             compiler_params=pltpu.CompilerParams(
-                collective_id=0, has_side_effects=True, vmem_limit_bytes=56 * 2**20
+                collective_id=0, has_side_effects=True, vmem_limit_bytes=48 * 2**20
             ),
         )(
             group_ids,

time: 134 us -> 115 us (0.86)
  Pallas kernels: 125 us -> 109 us
  local copies, waits for them, and re-layouts: 8.58 us -> 4.94 us
    pallas_call x1, Pallas kernels: 125 us -> 109 us  [on_device(): pl.pallas_call(functools.partial(kernel, n, mp, width), out_shape=(pltpu....]
    unnamed x10 -> x4, local copies, waits for them, and re-layouts: 8.58 us -> 4.94 us
where the time goes in v2:
time: 115 us
  Pallas kernels  109 us (95%)
  local copies, waits for them, and re-layouts  4.94 us (4%)
    pallas_call x1, Pallas kernels, on_device(): pl.pallas_call(functools.partial(kernel, n, mp, width), out_shape=(pltpu....  109 us
    unnamed x4, local copies, waits for them, and re-layouts  4.94 us

profile of v2, /device:TPU:0, one launch (start us, length us, event | category | flops | bytes accessed | tf_op | source)
XLA Modules:
  0.0 115.1 jit_solution(10640639444705928325)
XLA Ops:
  0.6 109.5 %shard_map.93 = (bf16[32,16,6144]{2,1,0:T(8,128)(2,1)S(1)}, f32[16,6144]{1,0:T(8,128)S(1)}, f32[16,6144]{1,0:T(8,128)S(1)}, f32[16,6144]{1,0:T(8,128)S(1)}) custom-call(s32[512]{0:T(512)} %ids_ref.1, bf16[16,2,16,6144]{3,2,1,0:T(8,128)(2,1)} %bitcast.4, bf16[32,16,6144]{2,1,0:T(8,128)(2,1)} %bitcast.5, f32[16,6144]{1,0:T(8,128)} %master_ref.1, ...), custom_call_target="tpu_custom_call" | custom-call | tf_op jit(solution)/shard_map/pallas_call | solution.py:238
  110.1 2.7 %copy.14 = bf16[512,6144]{1,0:T(8,128)(2,1)} copy(bf16[512,6144]{1,0:T(8,128)(2,1)S(1)} %bitcast.3) | data formatting | bytes 12582912
  112.8 0.7 copy.15
  113.6 0.7 copy.16
  114.3 0.7 copy.17
